TPU v7x, 256 devices: a whole 4x4x8 slice. The times are simulated.
256 devices in a mesh: section: 8 (over y, core), mp: 32 (over x, z).
Axes of the slice: x: 4, y: 4, z: 8, core: 2. Of those that a mesh axis runs over, the one named last changes fastest.
Arguments:
- arriving: bfloat16 [8, 768, 8192], P('section', None, 'mp'), may hold values from -6 to 6
- norm_gain: bfloat16 [8, 8192], P('section'), may hold values from 0.099609375 to 1.8984375
- w_query: bfloat16 [8, 8192, 8192], P('section', 'mp'), may hold values from -26 to 26
- w_key: bfloat16 [8, 1024, 8192], P('section', 'mp'), may hold values from -1 to 1
- w_value: bfloat16 [8, 1024, 8192], P('section', 'mp'), may hold values from -0.25 to 0.25
- w_out: bfloat16 [8, 8192, 8192], P('section', 'mp'), may hold values from -0.0625 to 0.0625
Outputs:
- attended: bfloat16 [8, 768, 8192], P('section', 'mp')
- stream_next: bfloat16 [8, 768, 8192], P('section', 'mp')
All inputs are finite; a program needn't handle non-finite values.
Results may differ from a plain program's by a relative error of at most 0.017.
Values may be sent and summed in bfloat16 or wider, within the bound.
A program may use at most 128 MiB of HBM per device.

v0:
```python
import math
import jax
import jax.numpy as jnp
from jax import lax
from jax.sharding import Mesh
from jax.sharding import PartitionSpec as P

HD = 128
KV_HEADS = 8
MP = ("mp_0", "mp_1")
rope_base = 500000.0
norm_eps = 1e-05


def shifted(block, axis, distance):
    devices = range(lax.axis_size(axis))
    route = [((i - distance) % len(devices), i) for i in devices]
    return lax.ppermute(block, axis, route)


def sent_together(arrays, axis, dim, along):
    both = jnp.concatenate(arrays, axis=along)
    result, at, outs = (lax.all_gather(both, axis, axis=dim, tiled=True), 0, [])
    for a in arrays:
        outs.append(lax.slice_in_dim(result, at, at + a.shape[along], axis=along))
        at += a.shape[along]
    return tuple(outs)


def scatter_axes(array, axes, dim):
    for axis in axes:
        array = lax.psum_scatter(array, axis, scatter_dimension=dim, tiled=True)
    return array


def rotate_pairs(channel_major, pair_ids):
    channels = channel_major.shape[0]
    length = channel_major.shape[1]
    frequency = jnp.exp(pair_ids.astype(jnp.float32) * (-2.0 * math.log(rope_base) / HD))
    positions = jnp.arange(length, dtype=jnp.int32).astype(jnp.float32)
    angles = frequency[:, None] * positions[None, :]
    cos_table = jnp.cos(angles)
    sine_table = jnp.sin(angles)
    paired = channel_major.reshape(channels // 2, 2, length)
    even_part = paired[:, 0]
    odd_part = paired[:, 1]
    rotated = jnp.stack(
        [
            even_part * cos_table - odd_part * sine_table,
            even_part * sine_table + odd_part * cos_table,
        ],
        axis=1,
    )
    return rotated.reshape(channels, length)


def head_rows(table, kv_index):
    length = table.shape[1]
    grouped = table.reshape(HD // 2, KV_HEADS, 2, length)
    picked = lax.dynamic_slice_in_dim(grouped, kv_index, 1, 1)
    return picked.reshape(HD, length)


def normalize(hidden_in, gain_row):
    as_float = hidden_in.astype(jnp.float32)
    mean_square = jnp.mean(as_float * as_float, axis=1, keepdims=True)
    normed = (as_float * lax.rsqrt(mean_square + norm_eps) * gain_row).astype(jnp.bfloat16)
    return (as_float, normed)


def channel_product(weights, normed):
    return lax.dot_general(
        weights, normed, (((1,), (1,)), ((), ())), preferred_element_type=jnp.float32
    )


def local(arriving, norm_gain, w_query, w_key, w_value, w_out):
    local_block = arriving[0]
    gain_row = norm_gain[0].astype(jnp.float32)
    query_weights = w_query[0]
    key_weights = w_key[0]
    value_weights = w_value[0]
    out_weights = w_out[0]
    mp_count = lax.axis_size(MP)
    member = lax.axis_index(MP)
    length = local_block.shape[0]
    row_count = length // mp_count
    arrived = shifted(local_block, "section", 1)
    whole_rows = lax.all_gather(arrived, MP, axis=1, tiled=True)
    full_float, normed_all = normalize(whole_rows, gain_row)
    residual = lax.dynamic_slice_in_dim(full_float, member * row_count, row_count, 0)
    projected = jnp.concatenate(
        [
            channel_product(query_weights, normed_all),
            channel_product(key_weights, normed_all),
            channel_product(value_weights, normed_all),
        ],
        axis=0,
    )
    q_width = query_weights.shape[0]
    k_width = key_weights.shape[0]
    query_pairs = jnp.arange(q_width // 2, dtype=jnp.int32) * 2 % HD // 2
    query_part = rotate_pairs(projected[:q_width], query_pairs).astype(jnp.bfloat16)
    key_pairs = (member * k_width + jnp.arange(k_width // 2, dtype=jnp.int32) * 2) // (2 * KV_HEADS)
    key_part = rotate_pairs(projected[q_width : q_width + k_width], key_pairs).astype(jnp.bfloat16)
    value_part = projected[q_width + k_width :].astype(jnp.bfloat16)
    key_all, value_all = sent_together((key_part, value_part), MP, 0, 1)
    local_heads = q_width // HD
    group_size = local_heads * mp_count // KV_HEADS
    kv_index = member * local_heads // group_size
    key_head = head_rows(key_all, kv_index)
    value_head = head_rows(value_all, kv_index)
    query_heads = query_part.reshape(local_heads, HD, length)
    score_scale = 1.0 / math.sqrt(HD)
    scores = (
        jnp.einsum("hdi,dj->hij", query_heads, key_head, preferred_element_type=jnp.float32)
        * score_scale
    )
    token_index = jnp.arange(length, dtype=jnp.int32)
    causal = token_index[:, None] >= token_index[None, :]
    scores = jnp.where(causal[None], scores, -1e30)
    row_max = jnp.max(scores, axis=-1, keepdims=True)
    exponent = jnp.exp(scores - row_max)
    row_total = jnp.sum(exponent, axis=-1, keepdims=True)
    weights = (exponent / row_total).astype(jnp.bfloat16)
    context = jnp.einsum(
        "hij,dj->ihd", weights, value_head, preferred_element_type=jnp.float32
    ).astype(jnp.bfloat16)
    context = context.reshape(length, q_width)
    full_term = jnp.dot(context, out_weights, preferred_element_type=jnp.float32)
    summed = scatter_axes(full_term.astype(jnp.bfloat16), MP, 0).astype(jnp.float32)
    attended = summed.astype(jnp.bfloat16)[None]
    stream_next = (residual + summed).astype(jnp.bfloat16)[None]
    return (attended, stream_next)


def solution(mesh):
    finer = Mesh(mesh.devices.reshape(mesh.shape["section"], 4, 8), ("section", "mp_0", "mp_1"))
    return jax.shard_map(
        local,
        mesh=finer,
        in_specs=(
            P("section", None, MP),
            P("section", None),
            P("section", MP, None),
            P("section", MP, None),
            P("section", MP, None),
            P("section", MP, None),
        ),
        out_specs=(P("section", MP, None), P("section", MP, None)),
        check_vma=False,
    )
```

profile of v0, /device:TPU:6, one launch (start us, length us, event | category | flops | bytes accessed | tf_op | source)
XLA Modules:
  0.0 442.5 jit_solution(10435901316648829320)
XLA Ops:
  7.2 0.0 copy-start
  7.2 0.0 all-gather.3.cloned.1.call-start
  7.2 0.0 collective-permute-start
  7.3 8.6 %collective-permute-done = bf16[768,256]{1,0:T(8,128)(2,1)S(1)} collective-permute-done((bf16[768,256]{1,0:T(8,128)(2,1)}, bf16[768,256]{1,0:T(8,128)(2,1)S(1)}, u32[]{:S(2)}, u32[]{:S(2)}) %collective-permute-start) | collective-permute-done | bytes 393248 | tf_op jit(solution)/shard_map/ppermute | solution.py:18
  15.9 0.7 copy-done.5
  16.6 0.0 all-gather.3.cloned.1.call-update
  16.6 0.0 all-gather.5.cloned.1.call-start
  16.7 0.8 mul.219
  17.5 125.5 %all-gather.3.cloned.1.call-done = bf16[768,8192]{1,0:T(8,128)(2,1)} async-done(((bf16[768,256]{1,0:T(8,128)(2,1)}), bf16[768,8192]{1,0:T(8,128)(2,1)}) %all-gather.3.cloned.1.call-update) | async-done | bytes 12582928 | tf_op jit(solution)/shard_map/all_gather | solution.py:89
  143.0 7.1 %multiply_reduce_fusion = f32[768]{0:T(1024)S(1)} fusion(bf16[768,8192]{1,0:T(8,128)(2,1)} %all-gather.3.cloned.1.call-done), kind=kLoop, calls=%fused_computation.2 | loop fusion | flops 18873600 | bytes 12585984 | tf_op jit(solution)/shard_map/reduce_sum | solution.py:66
  150.1 7.5 %multiply_convert_fusion = bf16[768,8192]{1,0:T(8,128)(2,1)S(1)} fusion(f32[8192]{0:T(1024)S(1)} %bitcast.54, f32[768]{0:T(1024)S(1)} %add_rsqrt_fusion, bf16[768,8192]{1,0:T(8,128)(2,1)} %all-gather.3.cloned.1.call-done), kind=kLoop, calls=%fused_computation.1 | loop fusion | flops 25165824 | bytes 25201664 | tf_op jit(solution)/shard_map/convert_element_type | solution.py:67
  157.6 0.0 copy-start.4
  157.6 3.8 fusion.13
  161.4 0.7 copy-done.2
  162.1 3.8 convolution_bitcast_fusion
  165.9 0.1 reshape.281
  166.0 0.1 fusion.47
  166.1 0.3 fusion.39
  166.4 0.6 pad_maximum_fusion.1
  167.1 0.0 all-gather.5.cloned.1.call-update
  167.1 0.0 reduce-scatter.3.cloned.1.call-start
  167.2 0.2 iota_compare_fusion
  167.4 14.0 %fusion.9 = f32[256,768]{1,0:T(8,128)S(1)} fusion(bf16[768,8192]{1,0:T(8,128)(2,1)} %copy-done.2, bf16[1,256,8192]{2,1,0:T(8,128)(2,1)} %param.8), kind=kOutput, calls=%fused_computation.16 | convolution fusion | flops 3221225472 | bytes 17563648 | tf_op jit(solution)/shard_map/dot_general | solution.py:72
  181.4 0.5 reshape.284
  181.9 0.6 fusion.46
  182.5 1.7 fusion.23
  184.2 0.4 copy.21
  184.6 0.1 convert_element_type.92
  184.8 58.3 %all-gather.5.cloned.1.call-done = bf16[1024,1536]{1,0:T(8,128)(2,1)} async-done(((bf16[32,1536]{1,0:T(8,128)(2,1)}), bf16[1024,1536]{1,0:T(8,128)(2,1)}) %all-gather.5.cloned.1.call-update) | async-done | bytes 3145744 | tf_op jit(solution)/shard_map/all_gather | solution.py:23
  243.1 3.2 fusion.45
  246.3 4.5 %reshape.285 = bf16[64,8,2,768]{3,2,1,0:T(2,128)(2,1)} reshape(bf16[1024,768]{1,0:T(8,128)(2,1)} %get-tuple-element.2) | data formatting | bytes 3145728 | tf_op jit(solution)/shard_map/reshape | solution.py:59
  250.8 1.1 dynamic-slice_bitcast_fusion
  251.9 0.1 reshape.286
  252.0 1.5 reshape.282
  253.5 1.1 constant_dynamic-slice_fusion
  254.6 0.1 reshape.290
  254.7 3.8 fusion.48
  258.5 3.0 fusion.12
  261.5 0.6 copy-done.3
  262.1 6.4 %convolution_convert_fusion = bf16[768,8192]{1,0:T(8,128)(2,1)} fusion(bf16[768,256]{0,1:T(8,128)(2,1)S(1)} %bitcast.53, bf16[1,256,8192]{2,1,0:T(8,128)(2,1)S(1)} %copy-done.3), kind=kOutput, calls=%fused_computation.3 | convolution fusion | flops 3227516928 | bytes 17170432 | tf_op jit(solution)/shard_map/dot_general | solution.py:130
  268.5 0.0 reduce-scatter.3.cloned.1.call-update
  268.5 0.0 reduce-scatter.5.cloned.1.call-start
  268.6 113.6 %reduce-scatter.3.cloned.1.call-done = bf16[192,8192]{1,0:T(8,128)(2,1)} async-done(((bf16[768,8192]{1,0:T(8,128)(2,1)}), bf16[192,8192]{1,0:T(8,128)(2,1)}) %reduce-scatter.3.cloned.1.call-update) | async-done | bytes 3145744 | tf_op jit(solution)/shard_map/reduce_scatter | solution.py:32
  382.1 0.0 reduce-scatter.5.cloned.1.call-update
  382.2 0.0 copy-start.1
  382.2 14.2 %convert_element_type.84 = f32[768,8192]{1,0:T(8,128)} convert(bf16[768,8192]{1,0:T(8,128)(2,1)} %all-gather.3.cloned.1.call-done) | non-fusion elementwise | flops 6291456 | bytes 37748736 | tf_op jit(solution)/shard_map/convert_element_type | solution.py:65
  396.4 37.5 %reduce-scatter.5.cloned.1.call-done = bf16[24,8192]{1,0:T(8,128)(2,1)} async-done(((bf16[192,8192]{1,0:T(8,128)(2,1)}), bf16[24,8192]{1,0:T(8,128)(2,1)}) %reduce-scatter.5.cloned.1.call-update) | async-done | bytes 393232 | tf_op jit(solution)/shard_map/reduce_scatter | solution.py:32
  433.9 2.1 fusion.26
  (14 shorter events, 0.2 us)
Async XLA Ops:
  7.2 150.4 %copy-start = (bf16[1,32,8192]{2,1,0:T(8,128)(2,1)S(1)}, bf16[1,32,8192]{2,1,0:T(8,128)(2,1)}, u32[]{:S(2)}) copy-start(bf16[1,32,8192]{2,1,0:T(8,128)(2,1)} %param.10) | copy-start | bytes 1572868
  7.2 135.8 %all-gather.3.cloned.1.call-start = ((), (), s32[]{:S(2)}) async-start(), calls=%async_computation.2 | async-start | bytes 12976128 | tf_op jit(solution)/shard_map/all_gather | solution.py:89
  7.2 8.6 %collective-permute-start = (bf16[768,256]{1,0:T(8,128)(2,1)}, bf16[768,256]{1,0:T(8,128)(2,1)S(1)}, u32[]{:S(2)}, u32[]{:S(2)}) collective-permute-start(bf16[768,256]{1,0:T(8,128)(2,1)} %bitcast.55), channel_id=1, source_target_pairs={{224,0},{0,32},{32,64},{64,96},{96,128},{128,160},{160,192},{192,2... | collective-permute-start | bytes 1179656 | tf_op jit(solution)/shard_map/ppermute | solution.py:18
  15.9 0.7 copy-start.5
  16.6 226.5 %all-gather.5.cloned.1.call-start = ((), (), s32[]{:S(2)}) async-start(), calls=%async_computation.3 | async-start | bytes 3244032 | tf_op jit(solution)/shard_map/all_gather | solution.py:23
  157.6 4.5 %copy-start.2 = (bf16[768,8192]{1,0:T(8,128)(2,1)}, bf16[768,8192]{1,0:T(8,128)(2,1)S(1)}, u32[]{:S(2)}) copy-start(bf16[768,8192]{1,0:T(8,128)(2,1)S(1)} %multiply_convert_fusion) | copy-start | bytes 37748740
  157.6 4.5 %copy-start.4 = (bf16[1,32,8192]{2,1,0:T(8,128)(2,1)S(1)}, bf16[1,32,8192]{2,1,0:T(8,128)(2,1)}, u32[]{:S(2)}) copy-start(bf16[1,32,8192]{2,1,0:T(8,128)(2,1)} %param.9) | copy-start | bytes 1572868
  167.1 215.0 %reduce-scatter.3.cloned.1.call-start = ((), (), s32[]{:S(2)}) async-start(), calls=%async_computation.4 | async-start | bytes 15728640 | tf_op jit(solution)/shard_map/reduce_scatter | solution.py:32
  258.5 3.6 copy-start.3
  268.5 165.4 %reduce-scatter.5.cloned.1.call-start = ((), (), s32[]{:S(2)}) async-start(), calls=%async_computation.5 | async-start | bytes 3538944 | tf_op jit(solution)/shard_map/reduce_scatter | solution.py:32
  382.2 53.8 %copy-start.1 = (bf16[1,32,8192]{2,1,0:T(8,128)(2,1)S(1)}, bf16[1,32,8192]{2,1,0:T(8,128)(2,1)}, u32[]{:S(2)}) copy-start(bf16[1,32,8192]{2,1,0:T(8,128)(2,1)} %param.10) | copy-start | bytes 1572868
Sparse Core Ops, SparseCore 0:
  16.8 126.1 all-gather.2
  167.2 75.8 all-gather.4
  268.6 113.4 reduce-scatter.2
  385.1 48.7 reduce-scatter.4
where the time goes:
time: 443 us
  waiting for transfers between devices  344 us (78%)
  matrix products  34.9 us (8%)
  other arithmetic  34.5 us (8%)
  local copies, waits for them, and re-layouts  15.5 us (3%)
  between operations  14 us (3%)
    reduce_scatter x2, waiting for transfers between devices, scatter_axes(): array = lax.psum_scatter(array, axis, scatter_dimension=dim, tiled=True)  151 us
    all_gather x1, waiting for transfers between devices, local(): whole_rows = lax.all_gather(arrived, MP, axis=1, tiled=True)  125 us
    all_gather x1, waiting for transfers between devices, sent_together(): result, at, outs = (lax.all_gather(both, axis, axis=dim, tiled=True), 0, [])  58.3 us
    dot_general x3, matrix products, channel_product(): lax.dot_general(weights, normed, (((1,), (1,)), ((), ())), preferred_elem...  21.7 us
    convert_element_type x1, other arithmetic, normalize(): as_float = hidden_in.astype(jnp.float32)  14.2 us
  transfers between devices with their start and end apart: 5, of which 5 were waited for; matrix products, arithmetic and copies ran while one was open for 7% of the time, Pallas kernels for 0%

commit v1 on v0

--- a/solution.py
+++ b/solution.py
@@ -86,7 +86,9 @@
     length = local_block.shape[0]
     row_count = length // mp_count
     arrived = shifted(local_block, "section", 1)
-    whole_rows = lax.all_gather(arrived, MP, axis=1, tiled=True)
+    whole_rows = jnp.concatenate(
+        lax.all_to_all(jnp.stack([arrived] * lax.axis_size(MP)), MP, 0, 0), axis=1
+    )
     full_float, normed_all = normalize(whole_rows, gain_row)
     residual = lax.dynamic_slice_in_dim(full_float, member * row_count, row_count, 0)
     projected = jnp.concatenate(

time: 443 us -> 648 us (1.46)
  waiting for transfers between devices: 344 us -> 523 us
  local copies, waits for them, and re-layouts: 15.5 us -> 44.8 us
  starting transfers between devices: 0.18 us -> 12.1 us
  matrix products: 34.9 us -> 26.3 us
  other arithmetic: 34.5 us -> 26.8 us
    all_to_all x0 -> x1, waiting for transfers between devices: none -> 277 us  [local(): lax.all_to_all(jnp.stack([arrived] * lax.axis_size(MP)), MP, 0, 0)]
    all_gather x1 -> x0, waiting for transfers between devices: 125 us -> none  [local(): whole_rows = lax.all_gather(arrived, MP, axis=1, tiled=True)]
    all_gather x1, waiting for transfers between devices: 58.3 us -> 85.4 us  [sent_together(): result, at, outs = (lax.all_gather(both, axis, axis=dim, tiled=True), 0, [])]
    all_to_all x0 -> x1, local copies, waits for them, and re-layouts: none -> 16.7 us  [local(): lax.all_to_all(jnp.stack([arrived] * lax.axis_size(MP)), MP, 0, 0)]
    all_to_all x0 -> x1, starting transfers between devices: none -> 11.8 us  [local(): lax.all_to_all(jnp.stack([arrived] * lax.axis_size(MP)), MP, 0, 0)]
    dot_general x3, matrix products: 21.7 us -> 13.2 us  [channel_product(): lax.dot_general(weights, normed, (((1,), (1,)), ((), ())), preferred_elem...]
    convert_element_type x1 -> x0, other arithmetic: 7.47 us -> none  [normalize(): (as_float * lax.rsqrt(mean_square + norm_eps) * gain_row).astype(jnp.bflo...]
    another operation x2 -> x3, other arithmetic: 1.92 us -> 9.38 us
  transfers between devices with their start and end apart: 5 -> 5, of which waited for: 5 -> 5; matrix products, arithmetic and copies ran while one was open for 7% -> 4% of each run, Pallas kernels for 0% -> 0%
where the time goes in v1:
time: 648 us; the launch traced here: 647 us
  waiting for transfers between devices  523 us (81%)
  local copies, waits for them, and re-layouts  44.8 us (7%)
  other arithmetic  26.8 us (4%)
  matrix products  26.3 us (4%)
  between operations  14 us (2%)
  starting transfers between devices  12.1 us (2%)
    all_to_all x1, waiting for transfers between devices, local(): lax.all_to_all(jnp.stack([arrived] * lax.axis_size(MP)), MP, 0, 0)  277 us
    reduce_scatter x2, waiting for transfers between devices, scatter_axes(): array = lax.psum_scatter(array, axis, scatter_dimension=dim, tiled=True)  152 us
    all_gather x1, waiting for transfers between devices, sent_together(): result, at, outs = (lax.all_gather(both, axis, axis=dim, tiled=True), 0, [])  85.4 us
    all_to_all x1, local copies, waits for them, and re-layouts, local(): lax.all_to_all(jnp.stack([arrived] * lax.axis_size(MP)), MP, 0, 0)  16.7 us
    dot_general x3, matrix products, channel_product(): lax.dot_general(weights, normed, (((1,), (1,)), ((), ())), preferred_elem...  13.2 us
  transfers between devices with their start and end apart: 5, of which 5 were waited for; matrix products, arithmetic and copies ran while one was open for 4% of the time, Pallas kernels for 0%

profile of v1, /device:TPU:6, one launch (start us, length us, event | category | flops | bytes accessed | tf_op | source)
XLA Modules:
  0.0 647.3 jit_solution(18410520962318758692)
XLA Ops:
  7.2 0.0 copy-start
  7.2 0.0 collective-permute-start
  7.2 8.6 %collective-permute-done = bf16[768,256]{1,0:T(8,128)(2,1)S(1)} collective-permute-done((bf16[768,256]{1,0:T(8,128)(2,1)}, bf16[768,256]{1,0:T(8,128)(2,1)S(1)}, u32[]{:S(2)}, u32[]{:S(2)}) %collective-permute-start) | collective-permute-done | bytes 393248 | tf_op jit(solution)/shard_map/ppermute | solution.py:18
  15.8 6.0 stack.8
  21.8 11.8 %all-to-all-start = ((bf16[32,768,256]{2,1,0:T(8,128)(2,1)}), bf16[32,768,256]{2,1,0:T(8,128)(2,1)}, u32[]{:S(2)}, u32[]{:S(2)}) async-start(bf16[32,768,256]{2,1,0:T(8,128)(2,1)} %stack.8), calls=%async_computation | async-start | bytes 25165824 | tf_op jit(solution)/shard_map/all_to_all | solution.py:90
  33.6 0.0 all-gather.2.cloned.1.call-start
  33.6 0.1 convert_reduce_fusion
  33.8 277.0 %all-to-all-done = bf16[32,768,256]{2,1,0:T(8,128)(2,1)} async-done(((bf16[32,768,256]{2,1,0:T(8,128)(2,1)}), bf16[32,768,256]{2,1,0:T(8,128)(2,1)}, u32[]{:S(2)}, u32[]{:S(2)}) %all-to-all-start) | async-done | bytes 12582944 | tf_op jit(solution)/shard_map/all_to_all | solution.py:90
  310.8 16.7 %copy.27 = bf16[32,768,256]{1,2,0:T(8,128)(2,1)} copy(bf16[32,768,256]{2,1,0:T(8,128)(2,1)} %all-to-all-done) | data formatting | bytes 25165824 | tf_op jit(solution)/shard_map/all_to_all | solution.py:90
  327.4 7.4 %multiply_reduce_fusion = f32[768]{0:T(1024)S(1)} fusion(bf16[32,768,256]{1,2,0:T(8,128)(2,1)} %copy.27), kind=kLoop, calls=%fused_computation.2 | loop fusion | flops 18873600 | bytes 12585984 | tf_op jit(solution)/shard_map/reduce_sum | solution.py:66
  334.9 7.5 %multiply_convert_fusion = bf16[32,768,256]{1,2,0:T(8,128)(2,1)S(1)} fusion(f32[32,256]{1,0:T(8,128)S(1)} %reshape.328, f32[768]{0:T(1024)S(1)} %add_rsqrt_fusion, bf16[32,768,256]{1,2,0:T(8,128)(2,1)} %copy.27), kind=kLoop, calls=%fused_computation.1 | loop fusion | flops 25165824 | bytes 25201664 | tf_op jit(solution)/shard_map/convert.7
  342.3 2.2 fusion.13
  344.5 2.2 copy-done.2
  346.8 2.2 convolution_bitcast_fusion
  349.0 0.1 reshape.321
  349.1 0.1 fusion.47
  349.1 0.3 fusion.39
  349.5 0.6 pad_maximum_fusion.1
  350.2 0.0 all-gather.2.cloned.1.call-update
  350.2 0.2 reduce-scatter.3.cloned.1.call-start
  350.5 0.2 iota_compare_fusion
  350.6 8.8 %fusion.9 = f32[256,768]{1,0:T(8,128)S(1)} fusion(bf16[768,8192]{0,1:T(8,128)(2,1)} %bitcast.59, bf16[1,256,8192]{2,1,0:T(8,128)(2,1)} %param.8), kind=kOutput, calls=%fused_computation.16 | convolution fusion | flops 3221225472 | bytes 17563648 | tf_op jit(solution)/shard_map/dot_general | solution.py:72
  359.5 0.5 reshape.324
  360.0 0.6 fusion.46
  360.6 1.7 fusion.23
  362.3 0.4 copy.33
  362.7 0.1 convert_element_type.108
  362.9 85.4 %all-gather.2.cloned.1.call-done = bf16[1024,1536]{1,0:T(8,128)(2,1)} async-done(((bf16[32,1536]{1,0:T(8,128)(2,1)}), bf16[1024,1536]{1,0:T(8,128)(2,1)}) %all-gather.2.cloned.1.call-update) | async-done | bytes 3145744 | tf_op jit(solution)/shard_map/all_gather | solution.py:23
  448.3 3.3 fusion.45
  451.5 4.5 reshape.325
  456.1 1.1 dynamic-slice_bitcast_fusion
  457.1 0.1 reshape.326
  457.2 1.5 reshape.322
  458.7 1.1 constant_dynamic-slice_fusion.1
  459.8 0.1 reshape.331
  459.9 3.8 fusion.48
  463.6 3.0 fusion.12
  466.6 0.6 copy-done.3
  467.2 6.3 convolution_convert_fusion
  473.6 0.0 reduce-scatter.3.cloned.1.call-update
  473.6 0.0 reduce-scatter.5.cloned.1.call-start
  473.7 113.6 %reduce-scatter.3.cloned.1.call-done = bf16[192,8192]{1,0:T(8,128)(2,1)} async-done(((bf16[768,8192]{1,0:T(8,128)(2,1)}), bf16[192,8192]{1,0:T(8,128)(2,1)}) %reduce-scatter.3.cloned.1.call-update) | async-done | bytes 3145744 | tf_op jit(solution)/shard_map/reduce_scatter | solution.py:32
  587.2 0.0 reduce-scatter.5.cloned.1.call-update
  587.2 7.1 %convert_element_type.100 = f32[32,768,256]{1,2,0:T(8,128)S(1)} convert(bf16[32,768,256]{1,2,0:T(8,128)(2,1)} %copy.27) | non-fusion elementwise | flops 6291456 | bytes 37748736 | tf_op jit(solution)/shard_map/convert_element_type | solution.py:65
  594.4 3.1 constant_dynamic-slice_fusion
  597.5 2.8 copy.47
  600.3 38.7 %reduce-scatter.5.cloned.1.call-done = bf16[24,8192]{1,0:T(8,128)(2,1)} async-done(((bf16[192,8192]{1,0:T(8,128)(2,1)}), bf16[24,8192]{1,0:T(8,128)(2,1)}) %reduce-scatter.5.cloned.1.call-update) | async-done | bytes 393232 | tf_op jit(solution)/shard_map/reduce_scatter | solution.py:32
  639.0 1.8 fusion.26
  (18 shorter events, 0.2 us)
Async XLA Ops:
  7.2 335.2 %copy-start = (bf16[1,32,8192]{2,1,0:T(8,128)(2,1)S(1)}, bf16[1,32,8192]{2,1,0:T(8,128)(2,1)}, u32[]{:S(2)}) copy-start(bf16[1,32,8192]{2,1,0:T(8,128)(2,1)} %param.10) | copy-start | bytes 1572868
  7.2 8.6 %collective-permute-start = (bf16[768,256]{1,0:T(8,128)(2,1)}, bf16[768,256]{1,0:T(8,128)(2,1)S(1)}, u32[]{:S(2)}, u32[]{:S(2)}) collective-permute-start(bf16[768,256]{1,0:T(8,128)(2,1)} %bitcast.63), channel_id=1, source_target_pairs={{224,0},{0,32},{32,64},{64,96},{96,128},{128,160},{160,192},{192,2... | collective-permute-start | bytes 1179656 | tf_op jit(solution)/shard_map/ppermute | solution.py:18
  21.8 11.8 %copy-start.5 = (bf16[1,8192]{1,0:T(2,128)(2,1)S(1)}, bf16[1,8192]{1,0:T(2,128)(2,1)}, u32[]{:S(2)}) copy-start(bf16[1,8192]{1,0:T(2,128)(2,1)} %param.7) | copy-start | bytes 49156
  21.8 289.0 %all-to-all-start = ((bf16[32,768,256]{2,1,0:T(8,128)(2,1)}), bf16[32,768,256]{2,1,0:T(8,128)(2,1)}, u32[]{:S(2)}, u32[]{:S(2)}) async-start(bf16[32,768,256]{2,1,0:T(8,128)(2,1)} %stack.8), calls=%async_computation | async-start | bytes 25165824 | tf_op jit(solution)/shard_map/all_to_all | solution.py:90
  33.6 414.7 %all-gather.2.cloned.1.call-start = ((), (), s32[]{:S(2)}) async-start(), calls=%async_computation.3 | async-start | bytes 3244032 | tf_op jit(solution)/shard_map/all_gather | solution.py:23
  342.3 4.5 copy-start.2
  342.3 4.5 copy-start.4
  350.2 237.0 %reduce-scatter.3.cloned.1.call-start = ((), (), s32[]{:S(2)}) async-start(), calls=%async_computation.4 | async-start | bytes 15728640 | tf_op jit(solution)/shard_map/reduce_scatter | solution.py:32
  463.6 3.6 copy-start.3
  473.6 165.4 %reduce-scatter.5.cloned.1.call-start = ((), (), s32[]{:S(2)}) async-start(), calls=%async_computation.5 | async-start | bytes 3538944 | tf_op jit(solution)/shard_map/reduce_scatter | solution.py:32
  594.4 46.4 %copy-start.1 = (bf16[1,32,8192]{2,1,0:T(8,128)(2,1)S(1)}, bf16[1,32,8192]{2,1,0:T(8,128)(2,1)}, u32[]{:S(2)}) copy-start(bf16[1,32,8192]{2,1,0:T(8,128)(2,1)} %param.10) | copy-start | bytes 1572868
Sparse Core Ops, SparseCore 0:
  350.3 97.9 all-gather.1
  473.7 113.4 reduce-scatter.2
  590.4 48.5 reduce-scatter.4
